TPU v7x, 128 devices: a whole 4x4x4 slice. The times are simulated.
128 devices in a mesh: group: 4 (over x_lo, core), bl: 32 (over x_hi, y, z).
Axes of the slice: x: 4 (x_hi: 2, x_lo: 2; x = x_hi * 2 + x_lo), y: 4, z: 4, core: 2. Of those that a mesh axis runs over, the one named last changes fastest.
Arguments:
- visibilities: float32 [2, 2048, 16, 1024], P(None, ('group', 'bl')), parts along dimension 1, may hold values from -400 to 400
- flags: int32 [2048, 8], P(('group', 'bl')), parts along dimension 0, may hold values 0 or 1
Outputs:
- cross_power: float32 [32, 2048, 512], P(None, ('group', 'bl')), parts along dimension 1
- bandpower: float32 [128], P('group'), parts along dimension 0
There are 4 independent parts, one for each index of `group`. A program takes and returns all parts, laid end to end along the dimension named above; each array names one. Nothing has to cross between parts.
All inputs are finite; a program needn't handle non-finite values. No bound on the sum of `flags` on one device may be relied on, other than what follows from the above.
Results may differ from a plain program's by a relative error of at most 0.004.
Values may be sent and summed in bfloat16 or wider, within the bound.
No kernel may reach another device: no remote copies, remote signals or barrier semaphores. Data moves between devices by JAX's collectives and lax.ppermute only.
A program may use at most 192 MiB of HBM per device.

v0:
```python
import math
import jax
import jax.numpy as jnp
from jax import lax
from jax.sharding import PartitionSpec as P

NF = 1024
NT = 16
CB = 128
BW = 32


def copy_for_each(array, axis):
    copies = jnp.broadcast_to(array, (lax.axis_size(axis), *array.shape))
    return lax.all_to_all(copies, axis, split_axis=0, concat_axis=0, tiled=True)


def taken_together(array, axis):
    return copy_for_each(array, axis).sum(axis=0)


def make_taper():
    angle = jnp.arange(NF, dtype=jnp.int32).astype(jnp.float32) * (2.0 * math.pi / (NF - 1))
    return (
        0.35875
        - 0.48829 * jnp.cos(angle)
        + 0.14128 * jnp.cos(2.0 * angle)
        - 0.01168 * jnp.cos(3.0 * angle)
    )


def make_tables():
    index = jnp.arange(NF, dtype=jnp.int32)
    phase = index[:, None] * index[None, :] % NF
    angle = phase.astype(jnp.float32) * (2.0 * math.pi / NF)
    return (jnp.cos(angle), jnp.sin(angle))


def delay_spectra(visibilities, flags):
    count = visibilities.shape[1]
    keep = (
        jnp.broadcast_to(flags[:, :, None], (count, NF // CB, CB))
        .reshape(count, NF)
        .astype(jnp.float32)
    )
    weight = keep * make_taper()[None, :]
    tapered = visibilities * weight[None, :, None, :]
    real_rows = tapered[0].reshape(count * NT, NF)
    imag_rows = tapered[1].reshape(count * NT, NF)
    cosine, sine = make_tables()
    high = lax.Precision.HIGHEST
    scale = 1.0 / math.sqrt(NF)
    real_out = (
        jnp.dot(real_rows, cosine, precision=high) + jnp.dot(imag_rows, sine, precision=high)
    ) * scale
    imag_out = (
        jnp.dot(imag_rows, cosine, precision=high) - jnp.dot(real_rows, sine, precision=high)
    ) * scale
    stacked = jnp.stack([real_out.reshape(count, NT, NF), imag_out.reshape(count, NT, NF)], 2)
    stacked = stacked.reshape(count, NT, 2, NF // BW, BW).transpose(3, 0, 1, 2, 4)
    return stacked.reshape(NF // BW, count, NT * 2 * BW).astype(jnp.bfloat16)


def shards(visibilities, flags):
    own = delay_spectra(visibilities, flags)
    bands, rows, inner = own.shape
    total = rows * lax.axis_size("bl")
    term = (
        jnp.einsum(
            "kbj,kcj->kbc",
            own,
            lax.all_gather(own, "bl", axis=1, tiled=True),
            preferred_element_type=jnp.float32,
        )
        / NT
    )
    own_wide = own.astype(jnp.float32)
    self_power = jnp.sum(own_wide * own_wide, axis=2) / NT
    partial_sum = jnp.sum(term, axis=(1, 2)) - jnp.sum(self_power, axis=1)
    bandpower = taken_together(partial_sum, "bl") / total
    return (term, bandpower)


def solution(mesh):
    return jax.shard_map(
        shards,
        mesh=mesh,
        in_specs=(P(None, ("group", "bl"), None, None), P(("group", "bl"), None)),
        out_specs=(P(None, ("group", "bl"), None), P("group")),
        check_vma=False,
    )
```

profile of v0, /device:TPU:0, one launch (start us, length us, event | category | flops | bytes accessed | tf_op | source)
XLA Modules:
  0.0 420.4 jit_solution(16420377505746367192)
XLA Ops:
  7.2 0.0 all-gather.2.cloned.1.call-start
  7.2 0.1 multiply_subtract_fusion
  7.3 0.7 convert_element_type.43
  8.0 0.1 copy.8
  8.0 0.1 broadcast_in_dim.4
  8.1 1.8 broadcast_multiply_fusion
  10.0 0.2 fusion.45
  10.2 20.0 %fusion.8 = f32[256,1024]{1,0:T(8,128)S(1)} fusion(f32[256,1024]{1,0:T(8,128)S(1)} %bitcast.14), kind=kOutput, calls=%fused_computation.13 | convolution fusion | flops 3235905536 | bytes 2097152 | tf_op jit(solution)/shard_map/dot_general | solution.py:57
  30.2 20.0 %fusion.10 = f32[256,1024]{1,0:T(8,128)S(1)} fusion(f32[256,1024]{1,0:T(8,128)S(1)} %bitcast.16), kind=kOutput, calls=%fused_computation.14 | convolution fusion | flops 3235905536 | bytes 2097152 | tf_op jit(solution)/shard_map/dot_general | solution.py:54
  50.2 19.7 %fusion.22 = bf16[256,1024]{1,0:T(8,128)(2,1)S(1)} fusion(f32[256,1024]{1,0:T(8,128)S(1)} %fusion.8, f32[256,1024]{1,0:T(8,128)S(1)} %bitcast.17), kind=kOutput, calls=%fused_computation.19 | convolution fusion | flops 3236691968 | bytes 2621440 | tf_op jit(solution)/shard_map/dot_general | solution.py:57
  70.0 19.5 %fusion.25 = bf16[256,1024]{1,0:T(8,128)(2,1)S(1)} fusion(f32[256,1024]{1,0:T(8,128)S(1)} %fusion.10, f32[256,1024]{1,0:T(8,128)S(1)} %bitcast.15), kind=kOutput, calls=%fused_computation.20 | convolution fusion | flops 3236691968 | bytes 2621440 | tf_op jit(solution)/shard_map/dot_general | solution.py:54
  89.5 1.6 stack.7
  91.1 2.6 stack.8
  93.7 4.5 %fusion.28 = bf16[32,16,16,2,32]{4,0,2,1,3:T(8,128)(2,1)} fusion(bf16[16,16,1,32,32]{4,3,1,0,2:T(8,128)(2,1)} %stack.8, bf16[16,16,1,32,32]{4,3,1,0,2:T(8,128)(2,1)S(1)} %stack.7), kind=kLoop, calls=%fused_computation.23 | loop fusion | flops 524288 | bytes 2097152 | tf_op jit(solution)/shard_map/convert_element_type | solution.py:61
  98.1 8.5 %copy.9 = bf16[32,16,16,2,32]{4,3,2,1,0:T(2,128)(2,1)} copy(bf16[32,16,16,2,32]{4,0,2,1,3:T(8,128)(2,1)} %fusion.28) | data formatting | bytes 2097152 | tf_op jit(solution)/shard_map/convert_element_type | solution.py:61
  106.6 11.7 %convert_element_type.49 = bf16[32,16,1024]{2,1,0:T(8,128)(2,1)} reshape(bf16[32,16,16,2,32]{4,3,2,1,0:T(2,128)(2,1)} %copy.9) | data formatting | bytes 2097152 | tf_op jit(solution)/shard_map/convert_element_type | solution.py:61
  118.4 0.0 copy-start
  118.4 0.0 all-gather.2.cloned.1.call-update
  118.4 2.8 multiply_reduce_fusion
  121.3 261.1 %all-gather.2.cloned.1.call-done = bf16[32,512,1024]{2,1,0:T(8,128)(2,1)} async-done(((bf16[32,16,1024]{2,1,0:T(8,128)(2,1)}), bf16[32,512,1024]{2,1,0:T(8,128)(2,1)}) %all-gather.2.cloned.1.call-update) | async-done | bytes 33554448 | tf_op jit(solution)/shard_map/all_gather | solution.py:72
  382.4 0.0 copy-done
  382.4 15.3 %fusion.46 = (f32[32]{0:T(128)S(1)}, f32[32,16,512]{2,1,0:T(8,128)}) fusion(bf16[32,16,1024]{2,1,0:T(8,128)(2,1)S(1)} %copy-done, bf16[32,512,1024]{2,1,0:T(8,128)(2,1)} %all-gather.2.cloned.1.call-done), kind=kOutput, calls=%fused_computation.45 | convolution fusion | flops 537395200 | bytes 35651712 | tf_op jit(solution)/shard_map/kbj,kcj->kbc/dot_general | solution.py:69
  397.7 15.3 %all_to_all.6 = f32[32,1,32]{2,1,0:T(1,128)S(1)} all-to-all(f32[32,1,32]{2,1,0:T(1,128)S(1)} %broadcast_in_dim.5), channel_id=1, replica_groups=mesh['group'=4,'bl'=32] {'bl'}, dimensions={0} | all-to-all | bytes 8192 | tf_op jit(solution)/shard_map/all_to_all | solution.py:15
  413.0 0.5 broadcast_multiply_fusion.1
  (5 shorter events, 0.1 us)
Async XLA Ops:
  7.2 375.2 %all-gather.2.cloned.1.call-start = ((), (), s32[]{:S(2)}) async-start(), calls=%async_computation.1 | async-start | bytes 34603008 | tf_op jit(solution)/shard_map/all_gather | solution.py:72
  118.4 264.0 %copy-start = (bf16[32,16,1024]{2,1,0:T(8,128)(2,1)S(1)}, bf16[32,16,1024]{2,1,0:T(8,128)(2,1)}, u32[]{:S(2)}) copy-start(bf16[32,16,1024]{2,1,0:T(8,128)(2,1)} %convert_element_type.49) | copy-start | bytes 3145732
Sparse Core Ops, SparseCore 0:
  118.5 263.7 all-gather.1
where the time goes:
time: 421 us; the launch traced here: 420 us
  waiting for transfers between devices  261 us (62%)
  matrix products  94.6 us (22%)
  local copies, waits for them, and re-layouts  24.8 us (6%)
  blocking collectives  15.3 us (4%)
  between operations  14.1 us (3%)
  other arithmetic  10.5 us (2%)
    all_gather x1, waiting for transfers between devices, shards(): lax.all_gather(own, 'bl', axis=1, tiled=True)  261 us
    convert_element_type x2, local copies, waits for them, and re-layouts, delay_spectra(): return stacked.reshape(NF // BW, count, NT * 2 * BW).astype(jnp.bfloat16)  20.2 us
    dot_general x1, matrix products, delay_spectra(): jnp.dot(imag_rows, cosine, precision=high)  20 us
    dot_general x1, matrix products, delay_spectra(): jnp.dot(real_rows, cosine, precision=high)  20 us
    dot_general x1, matrix products, delay_spectra(): jnp.dot(real_rows, sine, precision=high)  19.7 us
    dot_general x1, matrix products, delay_spectra(): jnp.dot(imag_rows, sine, precision=high)  19.5 us
    all_to_all x1, blocking collectives, copy_for_each(): return lax.all_to_all(copies, axis, split_axis=0, concat_axis=0, tiled=True)  15.3 us
    dot_general x1, matrix products, shards(): jnp.einsum('kbj,kcj->kbc', own, lax.all_gather(own, 'bl', axis=1, tiled=T...  15.3 us
  transfers between devices with their start and end apart: 1, of which 1 were waited for; matrix products, arithmetic and copies ran while one was open for 1% of the time, Pallas kernels for 0%

commit v1 on v0

--- a/solution.py
+++ b/solution.py
@@ -8,6 +8,11 @@
 NT = 16
 CB = 128
 BW = 32
+
+
+def gather_over(x, mesh_axis, along):
+    outgoing = jnp.stack([x] * lax.axis_size(mesh_axis))
+    return jnp.concatenate(lax.all_to_all(outgoing, mesh_axis, 0, 0), axis=along)
 
 
 def copy_for_each(array, axis):
@@ -67,10 +72,7 @@
     total = rows * lax.axis_size("bl")
     term = (
         jnp.einsum(
-            "kbj,kcj->kbc",
-            own,
-            lax.all_gather(own, "bl", axis=1, tiled=True),
-            preferred_element_type=jnp.float32,
+            "kbj,kcj->kbc", own, gather_over(own, "bl", 1), preferred_element_type=jnp.float32
         )
         / NT
     )

time: 421 us -> 776 us (1.84)
  waiting for transfers between devices: 261 us -> 525 us
  blocking collectives: 15.3 us -> 71.6 us
  local copies, waits for them, and re-layouts: 24.8 us -> 58 us
  between operations: 14.1 us -> 0.72 us
  starting transfers between devices: 0.04 us -> 11.3 us
    all_to_all x0 -> x1, waiting for transfers between devices: none -> 525 us  [gather_over(): lax.all_to_all(outgoing, mesh_axis, 0, 0)]
    all_gather x1 -> x0, waiting for transfers between devices: 261 us -> none  [shards(): lax.all_gather(own, 'bl', axis=1, tiled=True)]
    all_to_all x1, blocking collectives: 15.3 us -> 71.6 us  [copy_for_each(): return lax.all_to_all(copies, axis, split_axis=0, concat_axis=0, tiled=True)]
    reshape x0 -> x1, local copies, waits for them, and re-layouts: none -> 22.8 us  [gather_over(): jnp.concatenate(lax.all_to_all(outgoing, mesh_axis, 0, 0), axis=along)]
    all_to_all x0 -> x1, starting transfers between devices: none -> 11.3 us  [gather_over(): lax.all_to_all(outgoing, mesh_axis, 0, 0)]
    another operation x0 -> x1, local copies, waits for them, and re-layouts: none -> 11 us  [gather_over(): outgoing = jnp.stack([x] * lax.axis_size(mesh_axis))]
  transfers between devices with their start and end apart: 1 -> 1, of which waited for: 1 -> 1; matrix products, arithmetic and copies ran while one was open for 1% -> 0% of each run, Pallas kernels for 0% -> 0%
where the time goes in v1:
time: 776 us; the launch traced here: 771 us
  waiting for transfers between devices  525 us (68%)
  matrix products  94.6 us (12%)
  blocking collectives  71.6 us (9%)
  local copies, waits for them, and re-layouts  58 us (7%)
  starting transfers between devices  11.3 us (1%)
  other arithmetic  10.4 us (1%)
    all_to_all x1, waiting for transfers between devices, gather_over(): lax.all_to_all(outgoing, mesh_axis, 0, 0)  525 us
    all_to_all x1, blocking collectives, copy_for_each(): return lax.all_to_all(copies, axis, split_axis=0, concat_axis=0, tiled=True)  71.6 us
    reshape x1, local copies, waits for them, and re-layouts, gather_over(): jnp.concatenate(lax.all_to_all(outgoing, mesh_axis, 0, 0), axis=along)  22.8 us
    dot_general x1, matrix products, delay_spectra(): jnp.dot(real_rows, cosine, precision=high)  20 us
    dot_general x1, matrix products, delay_spectra(): jnp.dot(imag_rows, cosine, precision=high)  20 us
    dot_general x1, matrix products, delay_spectra(): jnp.dot(real_rows, sine, precision=high)  19.7 us
    dot_general x1, matrix products, delay_spectra(): jnp.dot(imag_rows, sine, precision=high)  19.5 us
    convert_element_type x2, local copies, waits for them, and re-layouts, delay_spectra(): return stacked.reshape(NF // BW, count, NT * 2 * BW).astype(jnp.bfloat16)  19.5 us
  transfers between devices with their start and end apart: 1, of which 1 were waited for; matrix products, arithmetic and copies ran while one was open for 0% of the time, Pallas kernels for 0%

profile of v1, /device:TPU:0, one launch (start us, length us, event | category | flops | bytes accessed | tf_op | source)
XLA Modules:
  0.0 771.0 jit_solution(12388866490129085089)
XLA Ops:
  0.6 0.1 multiply_subtract_fusion
  0.7 0.7 convert_element_type.45
  1.4 0.1 copy.12
  1.5 0.1 broadcast_in_dim.4
  1.6 1.8 broadcast_multiply_fusion
  3.4 0.2 fusion.45
  3.6 20.0 %fusion.8 = f32[256,1024]{1,0:T(8,128)S(1)} fusion(f32[256,1024]{1,0:T(8,128)S(1)} %bitcast.17), kind=kOutput, calls=%fused_computation.13 | convolution fusion | flops 3235905536 | bytes 2097152 | tf_op jit(solution)/shard_map/dot_general | solution.py:62
  23.6 20.0 %fusion.10 = f32[256,1024]{1,0:T(8,128)S(1)} fusion(f32[256,1024]{1,0:T(8,128)S(1)} %bitcast.19), kind=kOutput, calls=%fused_computation.14 | convolution fusion | flops 3235905536 | bytes 2097152 | tf_op jit(solution)/shard_map/dot_general | solution.py:59
  43.6 19.7 %fusion.22 = bf16[256,1024]{1,0:T(8,128)(2,1)S(1)} fusion(f32[256,1024]{1,0:T(8,128)S(1)} %fusion.8, f32[256,1024]{1,0:T(8,128)S(1)} %bitcast.20), kind=kOutput, calls=%fused_computation.19 | convolution fusion | flops 3236691968 | bytes 2621440 | tf_op jit(solution)/shard_map/dot_general | solution.py:62
  63.4 19.5 %fusion.25 = bf16[256,1024]{1,0:T(8,128)(2,1)S(1)} fusion(f32[256,1024]{1,0:T(8,128)S(1)} %fusion.10, f32[256,1024]{1,0:T(8,128)S(1)} %bitcast.18), kind=kOutput, calls=%fused_computation.20 | convolution fusion | flops 3236691968 | bytes 2621440 | tf_op jit(solution)/shard_map/dot_general | solution.py:59
  82.9 1.6 stack.8
  84.5 2.6 stack.9
  87.1 4.5 fusion.28
  91.6 8.5 %copy.13 = bf16[32,16,16,2,32]{4,3,2,1,0:T(2,128)(2,1)} copy(bf16[32,16,16,2,32]{4,0,2,1,3:T(8,128)(2,1)} %fusion.28) | data formatting | bytes 2097152 | tf_op jit(solution)/shard_map/convert_element_type | solution.py:66
  100.1 11.0 %convert_element_type.51 = bf16[32,16,1024]{2,1,0:T(8,128)(2,1)S(1)} reshape(bf16[32,16,16,2,32]{4,3,2,1,0:T(2,128)(2,1)} %copy.13) | data formatting | bytes 2097152 | tf_op jit(solution)/shard_map/convert_element_type | solution.py:66
  111.1 11.0 %stack.11 = bf16[32,32,16,1024]{3,2,1,0:T(8,128)(2,1)} broadcast(bf16[32,16,1024]{2,1,0:T(8,128)(2,1)S(1)} %convert_element_type.51), dimensions={1,2,3} | broadcast | bytes 34603008 | tf_op jit(solution)/shard_map/stack | solution.py:14
  122.1 11.3 %all-to-all-start = ((bf16[32,32,16,1024]{3,2,1,0:T(8,128)(2,1)}), bf16[32,32,16,1024]{3,2,1,0:T(8,128)(2,1)}, u32[]{:S(2)}, u32[]{:S(2)}) async-start(bf16[32,32,16,1024]{3,2,1,0:T(8,128)(2,1)} %stack.11), calls=%async_computation | async-start | bytes 67108864 | tf_op jit(solution)/shard_map/all_to_all | solution.py:15
  133.4 2.8 multiply_reduce_fusion
  136.2 524.6 %all-to-all-done = bf16[32,32,16,1024]{3,2,1,0:T(8,128)(2,1)} async-done(((bf16[32,32,16,1024]{3,2,1,0:T(8,128)(2,1)}), bf16[32,32,16,1024]{3,2,1,0:T(8,128)(2,1)}, u32[]{:S(2)}, u32[]{:S(2)}) %all-to-all-start) | async-done | bytes 33554464 | tf_op jit(solution)/shard_map/all_to_all | solution.py:15
  660.8 22.8 %copy.14 = bf16[32,32,16,1024]{3,2,1,0:T(8,128)(2,1)} copy(bf16[32,32,16,1024]{3,2,0,1:T(8,128)(2,1)} %bitcast.3) | data formatting | bytes 67108864 | tf_op jit(solution)/shard_map/reshape | solution.py:15
  683.6 15.3 %fusion.46 = (f32[32]{0:T(128)S(1)}, f32[32,16,512]{2,1,0:T(8,128)}) fusion(bf16[32,16,1024]{2,1,0:T(8,128)(2,1)S(1)} %convert_element_type.51, bf16[32,512,1024]{2,1,0:T(8,128)(2,1)} %bitcast.16), kind=kOutput, calls=%fused_computation.45 | convolution fusion | flops 537395200 | bytes 35651712 | tf_op jit(solution)/shard_map/kbj,kcj->kbc/dot_general | solution.py:74
  698.9 71.6 %all_to_all.11 = f32[32,1,32]{2,1,0:T(1,128)S(1)} all-to-all(f32[32,1,32]{2,1,0:T(1,128)S(1)} %broadcast_in_dim.5), channel_id=1, replica_groups=mesh['group'=4,'bl'=32] {'bl'}, dimensions={0} | all-to-all | bytes 8192 | tf_op jit(solution)/shard_map/all_to_all | solution.py:20
  770.5 0.5 broadcast_multiply_fusion.1
  (5 shorter events, 0.1 us)
Async XLA Ops:
  122.1 538.7 %all-to-all-start = ((bf16[32,32,16,1024]{3,2,1,0:T(8,128)(2,1)}), bf16[32,32,16,1024]{3,2,1,0:T(8,128)(2,1)}, u32[]{:S(2)}, u32[]{:S(2)}) async-start(bf16[32,32,16,1024]{3,2,1,0:T(8,128)(2,1)} %stack.11), calls=%async_computation | async-start | bytes 67108864 | tf_op jit(solution)/shard_map/all_to_all | solution.py:15
